TPU v7x, 32 devices: a whole 2x2x4 slice. The times are simulated.
32 devices in a mesh: replica: 8 (over y, x, core), mp: 4 (over z).
Axes of the slice: x: 2, y: 2, z: 4, core: 2. Of those that a mesh axis runs over, the one named last changes fastest.
Arguments:
- pseudo_grad: bfloat16 [8, 2, 3072, 2048], P('replica', None, None, 'mp'), may hold values from -6 to 6
- outer_params: float32 [2, 3072, 2048], P(None, 'replica', 'mp'), may hold values from -6 to 6
- momentum: float32 [2, 3072, 2048], P(None, 'replica', 'mp'), may hold values from -3 to 3
- acts: bfloat16 [1024, 3072], P('replica', 'mp'), may hold values from -6 to 6
- queries: bfloat16 [1024, 2048], P('replica', 'mp'), may hold values from -6 to 6
- keys: bfloat16 [1024, 2048], P('replica', 'mp'), may hold values from -6 to 6
- doc_ids: int32 [1024], P('replica'), may hold values from 0 to 31, never falling along the last dimension, each value on 1 to 64 neighbouring positions
Outputs:
- new_outer: float32 [2, 3072, 2048], P(None, 'replica', 'mp')
- new_momentum: float32 [2, 3072, 2048], P(None, 'replica', 'mp')
- new_local: bfloat16 [8, 3072, 2048], P('replica', None, 'mp')
Inputs may be any that keep to these rules, and one draw needn't show every extreme that they name: doc_ids never fall along the rows; each document covers 1 to 64 positions.
All inputs are finite; a program needn't handle non-finite values.
Results may differ from a plain program's by a relative error of at most 0.0037.
The roundings to bfloat16 on the way count: a program that leaves them out, or rounds other values in their place, can miss the bound.
Values may be sent and summed in bfloat16 or wider, within the bound.
A program may use at most 64 MiB of HBM per device.

v0:
```python
import jax
import jax.numpy as jnp
from jax import lax
from jax.sharding import PartitionSpec as P

HD = 256
norm_eps = 1e-06
outer_rate = 0.7
outer_beta = 0.9
inner_rate = 0.1


def attend(query, key_rows, value_rows, doc_rows):
    count = query.shape[0]
    scores = jnp.einsum(
        "qhd,khd->hqk", query, key_rows, preferred_element_type=jnp.float32
    ) * query.shape[2] ** (-0.5)
    row_pos = lax.broadcasted_iota(jnp.int32, (count, count), 0)
    col_pos = lax.broadcasted_iota(jnp.int32, (count, count), 1)
    allowed = (row_pos >= col_pos) & (doc_rows[:, None] == doc_rows[None, :])
    scores = jnp.where(allowed[None], scores, -1e30)
    probs = jax.nn.softmax(scores, axis=-1).astype(jnp.bfloat16)
    context = jnp.einsum("hqk,khd->qhd", probs, value_rows, preferred_element_type=jnp.float32)
    return context.astype(jnp.bfloat16)


def outer_update(summed, params_rows, moment_rows, workers):
    delta = summed / workers
    moment_next = outer_beta * moment_rows + delta
    params_next = params_rows - outer_rate * (delta + outer_beta * moment_next)
    return (params_next, moment_next)


def shards(pseudo_grad, outer_params, momentum, acts, queries, keys, doc_ids):
    workers = lax.axis_size("replica")
    groups = lax.axis_size("mp")
    full_x = lax.all_gather(acts, "mp", axis=1, tiled=True)
    blocks = lax.all_to_all(pseudo_grad, "replica", split_axis=2, concat_axis=0, tiled=True)
    summed = jnp.sum(blocks.astype(jnp.float32), axis=0)
    new_outer, new_momentum = outer_update(summed, outer_params, momentum, workers)
    weights = lax.all_gather(new_outer.astype(jnp.bfloat16), "replica", axis=1, tiled=True)
    count, width = full_x.shape
    cols = weights.shape[2]
    heads_here = cols // HD
    all_cols = cols * groups
    rows_f = full_x.astype(jnp.float32)
    normed = (
        rows_f * lax.rsqrt(jnp.mean(rows_f * rows_f, axis=-1, keepdims=True) + norm_eps)
    ).astype(jnp.bfloat16)
    values = (
        jnp.dot(normed, weights[0], preferred_element_type=jnp.float32) * width ** (-0.5)
    ).astype(jnp.bfloat16)
    query = queries.reshape(count, heads_here, HD)
    keyed = keys.reshape(count, heads_here, HD)

    def attn_fn(c):
        return attend(query, keyed, c, doc_ids)

    context, pullback = jax.vjp(attn_fn, values.reshape(count, heads_here, HD))
    ctx = context.reshape(count, cols)
    partial_branch = lax.dot_general(
        ctx, weights[1], (((1,), (1,)), ((), ())), preferred_element_type=jnp.float32
    ) * all_cols ** (-0.5)
    branch = lax.psum(partial_branch.astype(jnp.bfloat16), "mp").astype(jnp.float32)
    dout = (rows_f + branch - jnp.roll(rows_f, -1, axis=0)).astype(jnp.bfloat16)
    dctx = (
        jnp.dot(dout, weights[1], preferred_element_type=jnp.float32) * all_cols ** (-0.5)
    ).astype(jnp.bfloat16)
    pulled = pullback(dctx.reshape(count, heads_here, HD))[0]
    grad = lax.dot_general(
        normed,
        pulled.reshape(count, cols),
        (((0,), (0,)), ((), ())),
        preferred_element_type=jnp.float32,
    ) * width ** (-0.5)
    squares = lax.psum(jnp.sum(grad * grad), "mp")
    rms = jnp.sqrt(squares / (width * all_cols) + norm_eps)
    new_local = (weights[0].astype(jnp.float32) - inner_rate * grad / rms).astype(jnp.bfloat16)
    return (new_outer, new_momentum, new_local[None])


def solution(mesh):
    placed = (
        P("replica", None, None, "mp"),
        P(None, "replica", "mp"),
        P(None, "replica", "mp"),
        P("replica", "mp"),
        P("replica", "mp"),
        P("replica", "mp"),
        P("replica"),
    )
    return jax.shard_map(
        shards,
        mesh=mesh,
        in_specs=placed,
        out_specs=(P(None, "replica", "mp"), P(None, "replica", "mp"), P("replica", None, "mp")),
        check_vma=False,
    )
```

profile of v0, /device:TPU:0, one launch (start us, length us, event | category | flops | bytes accessed | tf_op | source)
XLA Modules:
  0.0 232.5 jit_solution(10670747100160510871)
XLA Ops:
  7.2 0.0 all-gather.2.cloned.1.call-start
  7.2 11.1 %copy.23 = bf16[1,2,3072,512]{3,1,0,2:T(2,128)(2,1)S(1)} copy(bf16[1,2,3072,512]{3,2,1,0:T(8,128)(2,1)} %param.7) | data formatting | bytes 12582912 | tf_op args[0]
  18.3 76.5 %all_to_all.4 = bf16[1,2,3072,512]{3,1,0,2:T(2,128)(2,1)S(1)} all-to-all(bf16[1,2,3072,512]{3,1,0,2:T(2,128)(2,1)S(1)} %copy.23), channel_id=1, replica_groups=mesh['replica'=8,'mp'=4] {'replica'}, dimensions={2} | all-to-all | bytes 12582912 | tf_op jit(solution)/shard_map/all_to_all | solution.py:38
  94.8 0.0 copy-start
  94.8 0.0 copy-start.1
  94.8 6.3 %convert_reduce_fusion = f32[2,384,512]{2,0,1:T(2,128)S(1)} fusion(bf16[2,8,384,512]{3,0,2,1:T(2,128)(2,1)S(1)} %bitcast.46), kind=kLoop, calls=%fused_computation.1 | loop fusion | flops 5898240 | bytes 7864320 | tf_op jit(solution)/shard_map/reduce_sum | solution.py:39
  101.1 0.0 copy-done
  101.1 0.0 copy-done.1
  101.1 0.0 copy-start.3
  101.1 0.0 copy-start.4
  101.1 0.0 copy-start.5
  101.1 0.0 copy-start.2
  101.1 2.7 %fusion.21 = (bf16[2,384,512]{2,1,0:T(8,128)(2,1)}, f32[2,384,512]{2,1,0:T(8,128)}, f32[2,384,512]{2,1,0:T(8,128)}) fusion(f32[2,384,512]{2,1,0:T(8,128)S(1)} %copy-done, f32[2,384,512]{2,0,1:T(2,128)S(1)} %convert_reduce_fusion, f32[2,384,512]{2,1,0:T(8,128)S(1)} %copy-done.1), kind=kLoop, calls=%fused_computation.38 | loop fusion | flops 3145728 | bytes 8650752 | tf_op jit(solution)/shard_map/convert_element_type | solution.py:41
  103.8 0.0 all-gather.2.cloned.1.call-update
  103.8 0.0 all-reduce.2.cloned.1.call-start
  103.9 0.0 copy-done.3
  103.9 0.1 fusion.19
  104.0 0.0 copy-done.4
  104.0 0.0 copy-done.5
  104.0 0.2 fusion.12
  104.2 0.1 fusion.22
  104.3 0.0 copy-done.2
  104.3 19.8 %all_gather.7 = bf16[128,3072]{1,0:T(8,128)(2,1)S(1)} all-gather(bf16[128,768]{1,0:T(8,128)(2,1)S(1)} %copy-done.2), channel_id=1, replica_groups=mesh['replica'=8,'mp'=4] {'mp'}, dimensions={1}, use_global_device_ids=true | all-gather | bytes 983040 | tf_op jit(solution)/shard_map/all_gather | solution.py:37
  124.1 0.2 multiply_reduce_fusion.1
  124.3 24.4 %all-gather.2.cloned.1.call-done = bf16[2,3072,512]{2,1,0:T(8,128)(2,1)} async-done(((bf16[2,384,512]{2,1,0:T(8,128)(2,1)}), bf16[2,3072,512]{2,1,0:T(8,128)(2,1)}) %all-gather.2.cloned.1.call-update) | async-done | bytes 6291472 | tf_op jit(solution)/shard_map/all_gather | solution.py:41
  148.7 2.5 %fusion.9 = bf16[128,512]{1,0:T(8,128)(2,1)S(1)} fusion(bf16[2,3072,512]{2,1,0:T(8,128)(2,1)} %all-gather.2.cloned.1.call-done, bf16[128,3072]{1,0:T(8,128)(2,1)S(1)} %all_gather.7, f32[128]{0:T(128)S(1)} %add_rsqrt_fusion), kind=kOutput, calls=%fused_computation.23 | convolution fusion | flops 403963904 | bytes 4063744 | tf_op jit(solution)/shard_map/dot_general | solution.py:51
  151.3 0.1 copy.33
  151.4 0.2 convolution_convert_fusion.1
  151.6 3.9 %fusion.1 = bf16[128,3072]{1,0:T(8,128)(2,1)} fusion(bf16[128,512]{0,1:T(8,128)(2,1)S(1)} %bitcast.52, bf16[2,3072,512]{2,1,0:T(8,128)(2,1)} %all-gather.2.cloned.1.call-done), kind=kOutput, calls=%fused_computation.5 | convolution fusion | flops 403439616 | bytes 4063232 | tf_op jit(solution)/shard_map/dot_general | solution.py:61
  155.5 0.0 all-reduce.2.cloned.1.call-update
  155.6 0.2 slice.22
  155.8 43.8 %all-reduce.2.cloned.1.call-done = bf16[128,3072]{1,0:T(8,128)(2,1)} async-done(((bf16[128,3072]{1,0:T(8,128)(2,1)}), bf16[128,3072]{1,0:T(8,128)(2,1)}) %all-reduce.2.cloned.1.call-update) | async-done | bytes 786448 | tf_op jit(solution)/shard_map/psum | solution.py:64
  199.6 2.8 %fusion.10 = bf16[128,512]{1,0:T(8,128)(2,1)S(1)} fusion(bf16[2,3072,512]{2,1,0:T(8,128)(2,1)} %all-gather.2.cloned.1.call-done, f32[1,3072]{1,0:T(1,128)S(1)} %slice.23, f32[127,3072]{1,0:T(8,128)S(1)} %slice.22, bf16[128,3072]{1,0:T(8,128)(2,1)} %all-reduce.2.cloned.1.call-done, bf16[128,3072]{1,0:T(8,128)(2,1)S(1)} %all_gather.7), kind=kOutput, calls=%fused_computation.24 | convolution fusion | flops 405143552 | bytes 6422528 | tf_op jit(solution)/shard_map/dot_general | solution.py:67
  202.4 0.1 copy.34
  202.5 0.2 convolution_convert_fusion
  202.7 5.1 %multiply_reduce_fusion = (f32[]{:T(128)}, f32[3072,512]{1,0:T(8,128)}) fusion(bf16[128,512]{0,1:T(8,128)(2,1)S(1)} %bitcast.47, bf16[128,3072]{1,0:T(8,128)(2,1)S(1)} %all_gather.7, f32[128]{0:T(128)S(1)} %add_rsqrt_fusion), kind=kOutput, calls=%fused_computation.3 | convolution fusion | flops 408551424 | bytes 7209476 | tf_op jit(solution)/shard_map/dot_general | solution.py:70
  207.8 10.6 %psum.15 = f32[]{:T(128)} all-reduce(f32[]{:T(128)} %get-tuple-element.6), channel_id=1, replica_groups=mesh['replica'=8,'mp'=4] {'mp'}, use_global_device_ids=true, to_apply=%region_6.7 | all-reduce | flops 1 | bytes 8 | tf_op jit(solution)/shard_map/psum | solution.py:76
  219.1 6.5 %fusion.2 = bf16[1,3072,512]{2,1,0:T(8,128)(2,1)} fusion(f32[]{:T(128)S(6)} %sqrt.3, f32[3072,512]{1,0:T(8,128)} %get-tuple-element.7, bf16[2,3072,512]{2,1,0:T(8,128)(2,1)} %all-gather.2.cloned.1.call-done), kind=kLoop, calls=%fused_computation.8 | loop fusion | flops 7864320 | bytes 12582916 | tf_op jit(solution)/shard_map/broadcast_in_dim | solution.py:79
  (2 shorter events, 0.0 us)
Async XLA Ops:
  7.2 141.6 %all-gather.2.cloned.1.call-start = ((), (), s32[]{:S(2)}) async-start(), calls=%async_computation.1 | async-start | bytes 7077888 | tf_op jit(solution)/shard_map/all_gather | solution.py:41
  94.8 6.3 %copy-start = (f32[2,384,512]{2,1,0:T(8,128)S(1)}, f32[2,384,512]{2,1,0:T(8,128)}, u32[]{:S(2)}) copy-start(f32[2,384,512]{2,1,0:T(8,128)} %param.8) | copy-start | bytes 4718596
  94.8 6.3 %copy-start.1 = (f32[2,384,512]{2,1,0:T(8,128)S(1)}, f32[2,384,512]{2,1,0:T(8,128)}, u32[]{:S(2)}) copy-start(f32[2,384,512]{2,1,0:T(8,128)} %param.9) | copy-start | bytes 4718596
  101.1 2.8 %copy-start.3 = (s32[128]{0:T(128)S(1)}, s32[128]{0:T(128)}, u32[]{:S(2)}) copy-start(s32[128]{0:T(128)} %param.13) | copy-start | bytes 1540
  101.1 2.9 %copy-start.4 = (bf16[128,512]{1,0:T(8,128)(2,1)S(1)}, bf16[128,512]{1,0:T(8,128)(2,1)}, u32[]{:S(2)}) copy-start(bf16[128,512]{1,0:T(8,128)(2,1)} %param.12) | copy-start | bytes 393220
  101.1 2.9 %copy-start.5 = (bf16[128,512]{1,0:T(8,128)(2,1)S(1)}, bf16[128,512]{1,0:T(8,128)(2,1)}, u32[]{:S(2)}) copy-start(bf16[128,512]{1,0:T(8,128)(2,1)} %param.11) | copy-start | bytes 393220
  101.1 3.1 %copy-start.2 = (bf16[128,768]{1,0:T(8,128)(2,1)S(1)}, bf16[128,768]{1,0:T(8,128)(2,1)}, u32[]{:S(2)}) copy-start(bf16[128,768]{1,0:T(8,128)(2,1)} %param.10) | copy-start | bytes 589828
  103.8 95.7 %all-reduce.2.cloned.1.call-start = ((), (), s32[]{:S(2)}) async-start(), calls=%async_computation.2 | async-start | bytes 1572864 | tf_op jit(solution)/shard_map/psum | solution.py:64
Sparse Core Ops, SparseCore 0:
  103.9 44.7 all-gather.1
  155.7 43.8 all-reduce.1
where the time goes:
time: 233 us; the launch traced here: 232 us
  blocking collectives  107 us (46%)
  waiting for transfers between devices  68.2 us (29%)
  other arithmetic  15.8 us (7%)
  matrix products  15 us (6%)
  between operations  14.9 us (6%)
  local copies, waits for them, and re-layouts  11.6 us (5%)
    all_to_all x1, blocking collectives, shards(): lax.all_to_all(pseudo_grad, 'replica', split_axis=2, concat_axis=0, tiled...  76.5 us
    psum x1, waiting for transfers between devices, shards(): lax.psum(partial_branch.astype(jnp.bfloat16), 'mp').astype(jnp.float32)  43.8 us
    all_gather x1, waiting for transfers between devices, shards(): lax.all_gather(new_outer.astype(jnp.bfloat16), 'replica', axis=1, tiled=T...  24.4 us
    all_gather x1, blocking collectives, shards(): full_x = lax.all_gather(acts, 'mp', axis=1, tiled=True)  19.8 us
    unnamed x13, local copies, waits for them, and re-layouts  11.1 us
    psum x1, blocking collectives, shards(): squares = lax.psum(jnp.sum(grad * grad), 'mp')  10.6 us
    broadcast_in_dim x1, other arithmetic, shards(): return (new_outer, new_momentum, new_local[None])  6.48 us
    reduce_sum x1, other arithmetic, shards(): summed = jnp.sum(blocks.astype(jnp.float32), axis=0)  6.26 us
  transfers between devices with their start and end apart: 2, of which 2 were waited for; matrix products, arithmetic and copies ran while one was open for 0% of the time, Pallas kernels for 0%

commit v1 on v0

--- a/solution.py
+++ b/solution.py
@@ -61,7 +61,9 @@
     partial_branch = lax.dot_general(
         ctx, weights[1], (((1,), (1,)), ((), ())), preferred_element_type=jnp.float32
     ) * all_cols ** (-0.5)
-    branch = lax.psum(partial_branch.astype(jnp.bfloat16), "mp").astype(jnp.float32)
+    branch = jnp.sum(lax.all_gather(partial_branch.astype(jnp.bfloat16), "mp"), axis=0).astype(
+        jnp.float32
+    )
     dout = (rows_f + branch - jnp.roll(rows_f, -1, axis=0)).astype(jnp.bfloat16)
     dctx = (
         jnp.dot(dout, weights[1], preferred_element_type=jnp.float32) * all_cols ** (-0.5)

time: 233 us -> 254 us (1.090)
  waiting for transfers between devices: 68.2 us -> 87.8 us
    all_gather x0 -> x1, waiting for transfers between devices: none -> 63.4 us  [shards(): lax.all_gather(partial_branch.astype(jnp.bfloat16), 'mp')]
    psum x1 -> x0, waiting for transfers between devices: 43.8 us -> none  [shards(): lax.psum(partial_branch.astype(jnp.bfloat16), 'mp').astype(jnp.float32)]
where the time goes in v1:
time: 254 us; the launch traced here: 253 us
  blocking collectives  106 us (42%)
  waiting for transfers between devices  87.8 us (35%)
  other arithmetic  18.3 us (7%)
  between operations  14.9 us (6%)
  matrix products  14.6 us (6%)
  local copies, waits for them, and re-layouts  11.6 us (5%)
    all_to_all x1, blocking collectives, shards(): lax.all_to_all(pseudo_grad, 'replica', split_axis=2, concat_axis=0, tiled...  76.5 us
    all_gather x1, waiting for transfers between devices, shards(): lax.all_gather(partial_branch.astype(jnp.bfloat16), 'mp')  63.4 us
    all_gather x1, waiting for transfers between devices, shards(): lax.all_gather(new_outer.astype(jnp.bfloat16), 'replica', axis=1, tiled=T...  24.4 us
    all_gather x1, blocking collectives, shards(): full_x = lax.all_gather(acts, 'mp', axis=1, tiled=True)  19.8 us
    unnamed x13, local copies, waits for them, and re-layouts  11.1 us
    psum x1, blocking collectives, shards(): squares = lax.psum(jnp.sum(grad * grad), 'mp')  9.7 us
    broadcast_in_dim x1, other arithmetic, shards(): return (new_outer, new_momentum, new_local[None])  6.48 us
    reduce_sum x1, other arithmetic, shards(): summed = jnp.sum(blocks.astype(jnp.float32), axis=0)  6.26 us
  transfers between devices with their start and end apart: 2, of which 2 were waited for; matrix products, arithmetic and copies ran while one was open for 0% of the time, Pallas kernels for 0%

profile of v1, /device:TPU:0, one launch (start us, length us, event | category | flops | bytes accessed | tf_op | source)
XLA Modules:
  0.0 253.3 jit_solution(14867964721753394341)
XLA Ops:
  7.2 0.0 all-gather.4.cloned.1.call-start
  7.2 11.1 %copy.23 = bf16[1,2,3072,512]{3,1,0,2:T(2,128)(2,1)S(1)} copy(bf16[1,2,3072,512]{3,2,1,0:T(8,128)(2,1)} %param.7) | data formatting | bytes 12582912 | tf_op args[0]
  18.3 76.5 %all_to_all.4 = bf16[1,2,3072,512]{3,1,0,2:T(2,128)(2,1)S(1)} all-to-all(bf16[1,2,3072,512]{3,1,0,2:T(2,128)(2,1)S(1)} %copy.23), channel_id=1, replica_groups=mesh['replica'=8,'mp'=4] {'replica'}, dimensions={2} | all-to-all | bytes 12582912 | tf_op jit(solution)/shard_map/all_to_all | solution.py:38
  94.8 0.0 copy-start
  94.8 0.0 copy-start.1
  94.8 6.3 %convert_reduce_fusion = f32[2,384,512]{2,0,1:T(2,128)S(1)} fusion(bf16[2,8,384,512]{3,0,2,1:T(2,128)(2,1)S(1)} %bitcast.47), kind=kLoop, calls=%fused_computation.1 | loop fusion | flops 5898240 | bytes 7864320 | tf_op jit(solution)/shard_map/reduce_sum | solution.py:39
  101.1 0.0 copy-done
  101.1 0.0 copy-done.1
  101.1 0.0 copy-start.3
  101.1 0.0 copy-start.4
  101.1 0.0 copy-start.5
  101.1 0.0 copy-start.2
  101.1 2.7 %fusion.21 = (bf16[2,384,512]{2,1,0:T(8,128)(2,1)}, f32[2,384,512]{2,1,0:T(8,128)}, f32[2,384,512]{2,1,0:T(8,128)}) fusion(f32[2,384,512]{2,1,0:T(8,128)S(1)} %copy-done, f32[2,384,512]{2,0,1:T(2,128)S(1)} %convert_reduce_fusion, f32[2,384,512]{2,1,0:T(8,128)S(1)} %copy-done.1), kind=kLoop, calls=%fused_computation.38 | loop fusion | flops 3145728 | bytes 8650752 | tf_op jit(solution)/shard_map/convert_element_type | solution.py:41
  103.8 0.0 all-gather.4.cloned.1.call-update
  103.8 0.0 all-gather.6.cloned.1.call-start
  103.9 0.0 copy-done.3
  103.9 0.1 fusion.19
  104.0 0.0 copy-done.4
  104.0 0.0 copy-done.5
  104.0 0.2 fusion.12
  104.2 0.1 fusion.22
  104.3 0.0 copy-done.2
  104.3 19.8 %all_gather.13 = bf16[128,3072]{1,0:T(8,128)(2,1)S(1)} all-gather(bf16[128,768]{1,0:T(8,128)(2,1)S(1)} %copy-done.2), channel_id=1, replica_groups=mesh['replica'=8,'mp'=4] {'mp'}, dimensions={1}, use_global_device_ids=true | all-gather | bytes 983040 | tf_op jit(solution)/shard_map/all_gather | solution.py:37
  124.1 0.2 multiply_reduce_fusion.1
  124.3 24.4 %all-gather.4.cloned.1.call-done = bf16[2,3072,512]{2,1,0:T(8,128)(2,1)} async-done(((bf16[2,384,512]{2,1,0:T(8,128)(2,1)}), bf16[2,3072,512]{2,1,0:T(8,128)(2,1)}) %all-gather.4.cloned.1.call-update) | async-done | bytes 6291472 | tf_op jit(solution)/shard_map/all_gather | solution.py:41
  148.7 2.5 fusion.9
  151.3 0.1 copy.33
  151.4 0.2 convolution_convert_fusion.1
  151.6 3.9 %fusion.1 = bf16[128,3072]{1,0:T(8,128)(2,1)} fusion(bf16[128,512]{0,1:T(8,128)(2,1)S(1)} %bitcast.54, bf16[2,3072,512]{2,1,0:T(8,128)(2,1)} %all-gather.4.cloned.1.call-done), kind=kOutput, calls=%fused_computation.5 | convolution fusion | flops 403439616 | bytes 4063232 | tf_op jit(solution)/shard_map/dot_general | solution.py:61
  155.5 0.0 all-gather.6.cloned.1.call-update
  155.6 0.2 slice.22
  155.8 63.4 %all-gather.6.cloned.1.call-done = bf16[512,3072]{1,0:T(8,128)(2,1)} async-done(((bf16[128,3072]{1,0:T(8,128)(2,1)}), bf16[512,3072]{1,0:T(8,128)(2,1)}) %all-gather.6.cloned.1.call-update) | async-done | bytes 3145744 | tf_op jit(solution)/shard_map/all_gather | solution.py:64
  219.2 2.5 reduce_sum.51
  221.7 2.5 fusion.10
  224.2 0.1 copy.34
  224.3 0.2 convolution_convert_fusion
  224.5 5.1 %multiply_reduce_fusion = (f32[]{:T(128)}, f32[3072,512]{1,0:T(8,128)}) fusion(bf16[128,512]{0,1:T(8,128)(2,1)S(1)} %bitcast.49, bf16[128,3072]{1,0:T(8,128)(2,1)S(1)} %all_gather.13, f32[128]{0:T(128)S(1)} %add_rsqrt_fusion), kind=kOutput, calls=%fused_computation.3 | convolution fusion | flops 408551424 | bytes 7209476 | tf_op jit(solution)/shard_map/dot_general | solution.py:72
  229.6 9.7 %psum.7 = f32[]{:T(128)} all-reduce(f32[]{:T(128)} %get-tuple-element.6), channel_id=1, replica_groups=mesh['replica'=8,'mp'=4] {'mp'}, use_global_device_ids=true, to_apply=%region_6.7 | all-reduce | flops 1 | bytes 8 | tf_op jit(solution)/shard_map/psum | solution.py:78
  240.0 6.5 %fusion.2 = bf16[1,3072,512]{2,1,0:T(8,128)(2,1)} fusion(f32[]{:T(128)S(6)} %sqrt.3, f32[3072,512]{1,0:T(8,128)} %get-tuple-element.7, bf16[2,3072,512]{2,1,0:T(8,128)(2,1)} %all-gather.4.cloned.1.call-done), kind=kLoop, calls=%fused_computation.8 | loop fusion | flops 7864320 | bytes 12582916 | tf_op jit(solution)/shard_map/broadcast_in_dim | solution.py:81
  (2 shorter events, 0.0 us)
Async XLA Ops:
  7.2 141.6 %all-gather.4.cloned.1.call-start = ((), (), s32[]{:S(2)}) async-start(), calls=%async_computation.1 | async-start | bytes 7077888 | tf_op jit(solution)/shard_map/all_gather | solution.py:41
  94.8 6.3 %copy-start = (f32[2,384,512]{2,1,0:T(8,128)S(1)}, f32[2,384,512]{2,1,0:T(8,128)}, u32[]{:S(2)}) copy-start(f32[2,384,512]{2,1,0:T(8,128)} %param.8) | copy-start | bytes 4718596
  94.8 6.3 %copy-start.1 = (f32[2,384,512]{2,1,0:T(8,128)S(1)}, f32[2,384,512]{2,1,0:T(8,128)}, u32[]{:S(2)}) copy-start(f32[2,384,512]{2,1,0:T(8,128)} %param.9) | copy-start | bytes 4718596
  101.1 2.8 %copy-start.3 = (s32[128]{0:T(128)S(1)}, s32[128]{0:T(128)}, u32[]{:S(2)}) copy-start(s32[128]{0:T(128)} %param.13) | copy-start | bytes 1540
  101.1 2.9 %copy-start.4 = (bf16[128,512]{1,0:T(8,128)(2,1)S(1)}, bf16[128,512]{1,0:T(8,128)(2,1)}, u32[]{:S(2)}) copy-start(bf16[128,512]{1,0:T(8,128)(2,1)} %param.12) | copy-start | bytes 393220
  101.1 2.9 %copy-start.5 = (bf16[128,512]{1,0:T(8,128)(2,1)S(1)}, bf16[128,512]{1,0:T(8,128)(2,1)}, u32[]{:S(2)}) copy-start(bf16[128,512]{1,0:T(8,128)(2,1)} %param.11) | copy-start | bytes 393220
  101.1 3.1 %copy-start.2 = (bf16[128,768]{1,0:T(8,128)(2,1)S(1)}, bf16[128,768]{1,0:T(8,128)(2,1)}, u32[]{:S(2)}) copy-start(bf16[128,768]{1,0:T(8,128)(2,1)} %param.10) | copy-start | bytes 589828
  103.8 115.3 %all-gather.6.cloned.1.call-start = ((), (), s32[]{:S(2)}) async-start(), calls=%async_computation.2 | async-start | bytes 3932160 | tf_op jit(solution)/shard_map/all_gather | solution.py:64
Sparse Core Ops, SparseCore 0:
  103.9 44.7 all-gather.3
  155.7 63.4 all-gather.5
